TPU v7x, 128 devices: a whole 4x4x4 slice. The times are simulated.
128 devices in a mesh: fsdp: 16 (over y_hi, z, core), tensor: 8 (over y_lo, x).
Axes of the slice: x: 4, y: 4 (y_hi: 2, y_lo: 2; y = y_hi * 2 + y_lo), z: 4, core: 2. Of those that a mesh axis runs over, the one named last changes fastest.
Arguments:
- states: bfloat16 [4096, 8192], P('fsdp'), may hold values from -64 to 64
- segment_ids: int32 [16, 256], P('fsdp'), may hold values from 0 to 3, never falling along the last dimension, each value on 1 to 128 neighbouring positions
- attn_gain: float32 [8192], replicated, may hold values from 0.1 to 1.9
- query_weight: bfloat16 [8192, 4096], P('fsdp', 'tensor'), may hold values from -2 to 2
- key_weight: bfloat16 [8192, 1024], P('fsdp', 'tensor'), may hold values from -2 to 2
- value_matrix: bfloat16 [8192, 1024], P('fsdp', 'tensor'), may hold values from -0.0625 to 0.0625
- out_weight: bfloat16 [4096, 8192], P('tensor', 'fsdp'), may hold values from -0.28125 to 0.28125
- final_gain: float32 [8192], P('tensor'), may hold values from 0.1 to 1.9
- head_weight: float32 [8192], P('tensor'), may hold values from -0.0625 to 0.0625
Outputs:
- scores: float32 [4096], P(('fsdp', 'tensor'))
- resid_out: bfloat16 [4096, 8192], P('fsdp', 'tensor')
Inputs may be any that keep to these rules, and one draw needn't show every extreme that they name: `segment_ids`: in each row, segment numbers never fall and each rollout spans 1 to 128 positions.
All inputs are finite; a program needn't handle non-finite values.
Results may differ from a plain program's by a relative error of at most 0.0071.
Values may be sent and summed in bfloat16 or wider, within the bound.
A program may use at most 128 MiB of HBM per device.

v0:
```python
import jax
import jax.numpy as jnp
from jax import lax
from jax.sharding import PartitionSpec as P

MODEL_WIDTH = 8192
HEAD_SIZE = 128
EPS = 1e-05
THETA = 500000.0
NEG_FILL = -1e30


def in_one_piece(arrays, axis, dim, along):
    both = jnp.concatenate(arrays, axis=along)
    result, at, outs = (lax.all_gather(both, axis, axis=dim, tiled=True), 0, [])
    for a in arrays:
        outs.append(lax.slice_in_dim(result, at, at + a.shape[along], axis=along))
        at += a.shape[along]
    return tuple(outs)


def sent_to_all(value, axis):
    length = lax.axis_size(axis)
    return lax.all_to_all(
        jnp.broadcast_to(value[None], (length, *value.shape)), axis, 0, 0, tiled=True
    )


def over_copies(value, axis):
    return sent_to_all(value, axis).sum(axis=0)


def together(arrays, axis):
    ravelled, at, outs = (jnp.concatenate([a.reshape(-1) for a in arrays]), 0, [])
    total = over_copies(ravelled, axis)
    for a in arrays:
        outs.append(total[at : at + a.size].reshape(a.shape))
        at += a.size
    return tuple(outs)


def rope_tables(seg_row):
    count = seg_row.shape[0]
    places = jnp.arange(count, dtype=jnp.int32)
    boundary = jnp.concatenate([jnp.ones((1,), dtype=bool), seg_row[1:] != seg_row[:-1]])
    begins = lax.cummax(jnp.where(boundary, places, jnp.zeros_like(places)), axis=0)
    positions = (places - begins).astype(jnp.float32)
    half_width = HEAD_SIZE // 2
    frequency = THETA ** (-(2.0 * jnp.arange(half_width, dtype=jnp.float32)) / HEAD_SIZE)
    angles = positions[:, None] * frequency[None, :]
    return (jnp.cos(angles), jnp.sin(angles))


def rotated(block, cosine, sine_part):
    half_width = block.shape[-1] // 2
    first_half = block[..., :half_width]
    second_half = block[..., half_width:]
    cos_rows = cosine[:, None, :]
    sin_rows = sine_part[:, None, :]
    return jnp.concatenate(
        [
            first_half * cos_rows - second_half * sin_rows,
            second_half * cos_rows + first_half * sin_rows,
        ],
        axis=-1,
    )


def attend(queries, key_rows, values, seg_row):
    t_rows = queries.shape[0]
    heads_here = queries.shape[1] // HEAD_SIZE
    groups_here = key_rows.shape[1] // HEAD_SIZE
    ratio = heads_here // groups_here
    cosine, sine_part = rope_tables(seg_row)
    query_rot = rotated(queries.reshape(t_rows, heads_here, HEAD_SIZE), cosine, sine_part).astype(
        jnp.bfloat16
    )
    key_rot = rotated(key_rows.reshape(t_rows, groups_here, HEAD_SIZE), cosine, sine_part).astype(
        jnp.bfloat16
    )
    value_rows = values.astype(jnp.bfloat16).reshape(t_rows, groups_here, HEAD_SIZE)
    grouped = query_rot.reshape(t_rows, groups_here, ratio, HEAD_SIZE)
    logits = jnp.einsum(
        "tkgd,skd->kgts", grouped, key_rot, preferred_element_type=jnp.float32
    ) * HEAD_SIZE ** (-0.5)
    places = jnp.arange(t_rows, dtype=jnp.int32)
    allowed = (seg_row[:, None] == seg_row[None, :]) & (places[None, :] <= places[:, None])
    logits = jnp.where(allowed[None, None], logits, NEG_FILL)
    row_peak = jnp.max(logits, axis=-1, keepdims=True)
    raised = jnp.exp(logits - row_peak)
    probabilities = (raised / jnp.sum(raised, axis=-1, keepdims=True)).astype(jnp.bfloat16)
    mixed = jnp.einsum(
        "kgts,skd->tkgd", probabilities, value_rows, preferred_element_type=jnp.float32
    )
    return mixed.astype(jnp.bfloat16).reshape(t_rows, heads_here * HEAD_SIZE)


def body(
    states,
    segment_ids,
    attn_gain,
    query_weight,
    key_weight,
    value_matrix,
    out_weight,
    final_gain,
    head_weight,
):
    t_rows, width = states.shape
    tensor_count = lax.axis_size("tensor")
    tensor_index = lax.axis_index("tensor")
    widened = states.astype(jnp.float32)
    normed = (
        widened
        * lax.rsqrt(jnp.sum(widened * widened, axis=1, keepdims=True) / MODEL_WIDTH + EPS)
        * attn_gain[None, :]
    ).astype(jnp.bfloat16)

    def add_piece(portion):
        return jnp.dot(normed, portion, preferred_element_type=jnp.float32)

    pieces = in_one_piece((query_weight, key_weight, value_matrix), "fsdp", 0, 1)
    queries = add_piece(pieces[0])
    key_rows = add_piece(pieces[1])
    values = add_piece(pieces[2])
    mixed = attend(queries, key_rows, values, segment_ids[0])
    slice_cols = width // tensor_count
    partials = jnp.dot(
        mixed,
        lax.all_gather(out_weight, "fsdp", axis=1, tiled=True),
        preferred_element_type=jnp.float32,
    )
    branch = lax.psum_scatter(partials, "tensor", scatter_dimension=1, tiled=True)
    own_cols = lax.dynamic_slice_in_dim(widened, tensor_index * slice_cols, slice_cols, 1)
    resid_out = (own_cols + branch).astype(jnp.bfloat16)
    stream = resid_out.astype(jnp.float32)
    squares = jnp.sum(stream * stream, axis=1)
    products = jnp.sum(stream * (final_gain * head_weight)[None, :], axis=1)
    share_rows = t_rows // tensor_count
    squares_all, products_all = together((squares, products), "tensor")
    local_squares = lax.dynamic_slice_in_dim(squares_all, tensor_index * share_rows, share_rows, 0)
    products_mine = lax.dynamic_slice_in_dim(products_all, tensor_index * share_rows, share_rows, 0)
    scores = products_mine * lax.rsqrt(local_squares / MODEL_WIDTH + EPS)
    return (scores, resid_out)


def solution(mesh):
    placed = (
        P("fsdp", None),
        P("fsdp", None),
        P(),
        P("fsdp", "tensor"),
        P("fsdp", "tensor"),
        P("fsdp", "tensor"),
        P("tensor", "fsdp"),
        P("tensor"),
        P("tensor"),
    )
    return jax.shard_map(
        body,
        mesh=mesh,
        in_specs=placed,
        out_specs=(P(("fsdp", "tensor")), P("fsdp", "tensor")),
        check_vma=False,
    )
```

profile of v0, /device:TPU:0, one launch (start us, length us, event | category | flops | bytes accessed | tf_op | source)
XLA Modules:
  0.0 299.0 jit_solution(9830881361931489665)
XLA Ops:
  7.2 2.1 pad_maximum_fusion
  9.4 0.7 all-gather.5.cloned.1.call-update
  10.2 0.8 compare_reduce_fusion
  11.1 0.3 reduce-window.9
  11.6 3.1 %multiply_reduce_fusion = f32[256]{0:T(256)S(1)} fusion(bf16[256,8192]{1,0:T(8,128)(2,1)} %param.9), kind=kLoop, calls=%fused_computation.3 | loop fusion | flops 6291200 | bytes 4195328 | tf_op jit(solution)/shard_map/reduce_sum | solution.py:115
  14.8 0.9 fusion.27
  15.7 0.5 multiply_cosine_fusion
  16.2 87.3 %all-gather.3.cloned.1.call-done = bf16[8192,768]{1,0:T(8,128)(2,1)} async-done(((bf16[512,768]{1,0:T(8,128)(2,1)}), bf16[8192,768]{1,0:T(8,128)(2,1)}) %all-gather.3.cloned.1.call-update) | async-done | bytes 12582928 | tf_op jit(solution)/shard_map/all_gather | solution.py:15
  103.6 7.1 %fusion = f32[256,512]{1,0:T(8,128)S(1)} fusion(bf16[8192,768]{1,0:T(8,128)(2,1)} %all-gather.3.cloned.1.call-done, f32[8192]{0:T(1024)} %param.11, f32[256]{0:T(256)S(1)} %add_rsqrt_fusion, bf16[256,8192]{1,0:T(8,128)(2,1)} %param.9), kind=kOutput, calls=%fused_computation | convolution fusion | flops 2155872256 | bytes 13140992 | tf_op jit(solution)/shard_map/dot_general | solution.py:120
  110.6 0.2 reshape.251
  110.8 4.9 %fusion.8 = f32[256,1,128]{0,2,1:T(8,128)S(1)} fusion(bf16[8192,768]{1,0:T(8,128)(2,1)} %all-gather.3.cloned.1.call-done, f32[8192]{0:T(1024)S(1)} %copy-done.2, f32[256]{0:T(256)S(1)} %add_rsqrt_fusion, bf16[256,8192]{1,0:T(8,128)(2,1)} %param.9), kind=kOutput, calls=%fused_computation.14 | convolution fusion | flops 545259520 | bytes 6456320 | tf_op jit(solution)/shard_map/dot_general | solution.py:120
  115.7 0.3 fusion.39
  116.0 0.3 fusion.43
  116.5 0.4 fusion.45
  117.1 4.6 %convolution_convert_fusion = bf16[128,4,256]{2,0,1:T(8,128)(2,1)S(1)} fusion(bf16[8192,768]{1,0:T(8,128)(2,1)} %all-gather.3.cloned.1.call-done, f32[1,4,256,256]{2,3,1,0:T(8,128)S(1)} %get-tuple-element.16, f32[4,256]{1,0:T(4,128)S(1)} %fusion.21, f32[4,256]{1,0:T(4,128)S(1)} %get-tuple-element.15, f32[8192]{0:T(1024)S(1)} %copy-done.2, ...), kind=kOutput, calls=%fused_computation.13 | convolution fusion | flops 613318656 | bytes 7644160 | tf_op jit(solution)/shard_map/kgts,skd->tkgd/dot_general | solution.py:92
  121.7 58.3 %all-gather.5.cloned.1.call-done = bf16[512,8192]{1,0:T(8,128)(2,1)} async-done(((bf16[512,512]{1,0:T(8,128)(2,1)}), bf16[512,8192]{1,0:T(8,128)(2,1)}) %all-gather.5.cloned.1.call-update) | async-done | bytes 8388624 | tf_op jit(solution)/shard_map/all_gather | solution.py:130
  180.0 9.0 %fusion.46 = f32[256,8192]{1,0:T(8,128)} fusion(bf16[256,512]{0,1:T(8,128)(2,1)S(1)} %bitcast.40, bf16[512,8192]{1,0:T(8,128)(2,1)} %all-gather.5.cloned.1.call-done), kind=kOutput, calls=%fused_computation.64 | convolution fusion | flops 2147483648 | bytes 17039360 | tf_op jit(solution)/shard_map/dot_general | solution.py:128
  189.1 6.7 %convert_element_type.41 = f32[256,8192]{1,0:T(8,128)} convert(bf16[256,8192]{1,0:T(8,128)(2,1)} %param.9) | non-fusion elementwise | flops 2097152 | bytes 12582912 | tf_op jit(solution)/shard_map/convert_element_type | solution.py:112
  195.7 83.5 %reduce-scatter.2.cloned.1.call-done = f32[256,1024]{1,0:T(8,128)} async-done(((f32[256,8192]{1,0:T(8,128)}), f32[256,1024]{1,0:T(8,128)}) %reduce-scatter.2.cloned.1.call-update) | async-done | bytes 1048592 | tf_op jit(solution)/shard_map/reduce_scatter | solution.py:133
  279.2 2.5 fusion.19
  281.8 0.6 broadcast_in_dim.15
  282.4 3.3 %all-to-all-start = ((f32[8,1,512]{2,1,0:T(1,128)}), f32[8,1,512]{2,1,0:T(1,128)S(1)}, u32[]{:S(2)}, u32[]{:S(2)}) async-start(f32[8,1,512]{2,1,0:T(1,128)} %broadcast_in_dim.15), calls=%async_computation.1 | async-start | bytes 32768 | tf_op jit(solution)/shard_map/all_to_all | solution.py:24
  285.7 6.1 %all-to-all-done = f32[8,1,512]{2,1,0:T(1,128)S(1)} async-done(((f32[8,1,512]{2,1,0:T(1,128)}), f32[8,1,512]{2,1,0:T(1,128)S(1)}, u32[]{:S(2)}, u32[]{:S(2)}) %all-to-all-start) | async-done | bytes 16416 | tf_op jit(solution)/shard_map/all_to_all | solution.py:24
  291.9 0.6 rsqrt_multiply_fusion
  (24 shorter events, 0.9 us)
Async XLA Ops:
  7.2 96.4 %all-gather.3.cloned.1.call-start = ((), (), s32[]{:S(2)}) async-start(), calls=%async_computation.2 | async-start | bytes 13369344 | tf_op jit(solution)/shard_map/all_gather | solution.py:15
  9.4 170.7 %all-gather.5.cloned.1.call-start = ((), (), s32[]{:S(2)}) async-start(), calls=%async_computation.3 | async-start | bytes 8912896 | tf_op jit(solution)/shard_map/all_gather | solution.py:130
  10.1 269.1 %reduce-scatter.2.cloned.1.call-start = ((), (), s32[]{:S(2)}) async-start(), calls=%async_computation.4 | async-start | bytes 9437184 | tf_op jit(solution)/shard_map/reduce_scatter | solution.py:133
  16.2 94.6 %copy-start.2 = (f32[8192]{0:T(1024)S(1)}, f32[8192]{0:T(1024)}, u32[]{:S(2)}) copy-start(f32[8192]{0:T(1024)} %param.11) | copy-start | bytes 98308
  189.0 6.7 %copy-start = (f32[1024]{0:T(1024)S(1)}, f32[1024]{0:T(1024)}, u32[]{:S(2)}) copy-start(f32[1024]{0:T(1024)} %param.16) | copy-start | bytes 12292
  189.1 6.7 %copy-start.1 = (f32[1024]{0:T(1024)S(1)}, f32[1024]{0:T(1024)}, u32[]{:S(2)}) copy-start(f32[1024]{0:T(1024)} %param.17) | copy-start | bytes 12292
  282.4 9.5 %all-to-all-start = ((f32[8,1,512]{2,1,0:T(1,128)}), f32[8,1,512]{2,1,0:T(1,128)S(1)}, u32[]{:S(2)}, u32[]{:S(2)}) async-start(f32[8,1,512]{2,1,0:T(1,128)} %broadcast_in_dim.15), calls=%async_computation.1 | async-start | bytes 32768 | tf_op jit(solution)/shard_map/all_to_all | solution.py:24
Sparse Core Ops, SparseCore 0:
  10.5 93.0 all-gather.2
  105.8 74.1 all-gather.4
  189.2 90.0 reduce-scatter.1
where the time goes:
time: 299 us
  waiting for transfers between devices  236 us (79%)
  matrix products  25.9 us (9%)
  other arithmetic  18.4 us (6%)
  between operations  13.9 us (5%)
  starting transfers between devices  3.45 us (1%)
    all_gather x1, waiting for transfers between devices, in_one_piece(): result, at, outs = (lax.all_gather(both, axis, axis=dim, tiled=True), 0, [])  87.3 us
    reduce_scatter x1, waiting for transfers between devices, body(): lax.psum_scatter(partials, 'tensor', scatter_dimension=1, tiled=True)  83.5 us
    all_gather x1, waiting for transfers between devices, body(): lax.all_gather(out_weight, 'fsdp', axis=1, tiled=True)  58.3 us
    dot_general x2, matrix products, add_piece(): return jnp.dot(normed, portion, preferred_element_type=jnp.float32)  11.9 us
    dot_general x1, matrix products, body(): jnp.dot(mixed, lax.all_gather(out_weight, 'fsdp', axis=1, tiled=True), pr...  8.98 us
    convert_element_type x1, other arithmetic, body(): widened = states.astype(jnp.float32)  6.65 us
    all_to_all x1, waiting for transfers between devices, sent_to_all(): lax.all_to_all(jnp.broadcast_to(value[None], (length, *value.shape)), axi...  6.14 us
  transfers between devices with their start and end apart: 4, of which 4 were waited for; matrix products, arithmetic and copies ran while one was open for 10% of the time, Pallas kernels for 0%

commit v1 on v0

--- a/solution.py
+++ b/solution.py
@@ -127,7 +127,7 @@
     slice_cols = width // tensor_count
     partials = jnp.dot(
         mixed,
-        lax.all_gather(out_weight, "fsdp", axis=1, tiled=True),
+        jnp.concatenate(lax.all_gather(out_weight, "fsdp"), axis=1),
         preferred_element_type=jnp.float32,
     )
     branch = lax.psum_scatter(partials, "tensor", scatter_dimension=1, tiled=True)

time: 299 us -> 314 us (1.050)
  local copies, waits for them, and re-layouts: 1.34 us -> 13.7 us
    reshape x0 -> x1, local copies, waits for them, and re-layouts: none -> 12.3 us  [body(): jnp.concatenate(lax.all_gather(out_weight, 'fsdp'), axis=1)]
    all_gather x1, waiting for transfers between devices: 58.3 us -> 69.5 us  [body(): lax.all_gather(out_weight, 'fsdp')]
    all_gather x1, waiting for transfers between devices: 87.3 us -> 78.4 us  [in_one_piece(): result, at, outs = (lax.all_gather(both, axis, axis=dim, tiled=True), 0, [])]
  transfers between devices with their start and end apart: 4 -> 4, of which waited for: 4 -> 4; matrix products, arithmetic and copies ran while one was open for 10% -> 9% of each run, Pallas kernels for 0% -> 0%
where the time goes in v1:
time: 314 us
  waiting for transfers between devices  239 us (76%)
  matrix products  25.7 us (8%)
  other arithmetic  18.3 us (6%)
  between operations  13.9 us (4%)
  local copies, waits for them, and re-layouts  13.7 us (4%)
  starting transfers between devices  3.45 us (1%)
    reduce_scatter x1, waiting for transfers between devices, body(): lax.psum_scatter(partials, 'tensor', scatter_dimension=1, tiled=True)  83.9 us
    all_gather x1, waiting for transfers between devices, in_one_piece(): result, at, outs = (lax.all_gather(both, axis, axis=dim, tiled=True), 0, [])  78.4 us
    all_gather x1, waiting for transfers between devices, body(): lax.all_gather(out_weight, 'fsdp')  69.5 us
    reshape x1, local copies, waits for them, and re-layouts, body(): jnp.concatenate(lax.all_gather(out_weight, 'fsdp'), axis=1)  12.3 us
    dot_general x2, matrix products, add_piece(): return jnp.dot(normed, portion, preferred_element_type=jnp.float32)  11.7 us
    dot_general x1, matrix products, body(): jnp.dot(mixed, jnp.concatenate(lax.all_gather(out_weight, 'fsdp'), axis=1...  9.02 us
    convert_element_type x1, other arithmetic, body(): widened = states.astype(jnp.float32)  6.46 us
  transfers between devices with their start and end apart: 4, of which 4 were waited for; matrix products, arithmetic and copies ran while one was open for 9% of the time, Pallas kernels for 0%

profile of v1, /device:TPU:0, one launch (start us, length us, event | category | flops | bytes accessed | tf_op | source)
XLA Modules:
  0.0 313.6 jit_solution(18242430141904869723)
XLA Ops:
  7.2 0.7 all-gather.6.cloned.1.call-update
  7.9 2.2 pad_maximum_fusion
  10.2 0.8 compare_reduce_fusion
  11.1 0.3 reduce-window.9
  11.7 3.1 multiply_reduce_fusion
  14.9 0.9 fusion.27
  15.7 0.5 multiply_cosine_fusion
  16.3 69.5 %all-gather.6.cloned.1.call-done = bf16[8192,512]{1,0:T(8,128)(2,1)} async-done(((bf16[512,512]{1,0:T(8,128)(2,1)}), bf16[8192,512]{1,0:T(8,128)(2,1)}) %all-gather.6.cloned.1.call-update) | async-done | bytes 8388624 | tf_op jit(solution)/shard_map/all_gather | solution.py:130
  85.8 12.3 %copy.36 = bf16[512,16,512]{0,2,1:T(8,128)(2,1)} copy(bf16[512,16,512]{2,0,1:T(8,128)(2,1)} %bitcast.45) | data formatting | bytes 16777216 | tf_op jit(solution)/shard_map/reshape | solution.py:130
  98.1 78.4 %all-gather.4.cloned.1.call-done = bf16[8192,768]{1,0:T(8,128)(2,1)} async-done(((bf16[512,768]{1,0:T(8,128)(2,1)}), bf16[8192,768]{1,0:T(8,128)(2,1)}) %all-gather.4.cloned.1.call-update) | async-done | bytes 12582928 | tf_op jit(solution)/shard_map/all_gather | solution.py:15
  176.6 7.0 %fusion = f32[256,512]{1,0:T(8,128)S(1)} fusion(bf16[8192,768]{1,0:T(8,128)(2,1)} %all-gather.4.cloned.1.call-done, f32[8192]{0:T(1024)S(1)} %copy-done.2, f32[256]{0:T(256)S(1)} %add_rsqrt_fusion, bf16[256,8192]{1,0:T(8,128)(2,1)} %param.9), kind=kOutput, calls=%fused_computation | convolution fusion | flops 2155872256 | bytes 13140992 | tf_op jit(solution)/shard_map/dot_general | solution.py:120
  183.8 0.3 fusion.43
  184.1 4.6 %fusion.8 = f32[256,1,128]{0,2,1:T(8,128)S(1)} fusion(bf16[8192,768]{1,0:T(8,128)(2,1)} %all-gather.4.cloned.1.call-done, f32[8192]{0:T(1024)S(1)} %copy-done.2, f32[256]{0:T(256)S(1)} %add_rsqrt_fusion, bf16[256,8192]{1,0:T(8,128)(2,1)} %param.9), kind=kOutput, calls=%fused_computation.14 | convolution fusion | flops 545259520 | bytes 6456320 | tf_op jit(solution)/shard_map/dot_general | solution.py:120
  188.7 0.3 fusion.39
  189.2 0.4 fusion.45
  189.8 4.6 %convolution_convert_fusion = bf16[128,4,256]{2,0,1:T(8,128)(2,1)S(1)} fusion(bf16[8192,768]{1,0:T(8,128)(2,1)} %all-gather.4.cloned.1.call-done, f32[1,4,256,256]{2,3,1,0:T(8,128)S(1)} %get-tuple-element.16, f32[4,256]{1,0:T(4,128)S(1)} %fusion.21, f32[4,256]{1,0:T(4,128)S(1)} %get-tuple-element.15, f32[8192]{0:T(1024)S(1)} %copy-done.2, ...), kind=kOutput, calls=%fused_computation.13 | convolution fusion | flops 613318656 | bytes 7644160 | tf_op jit(solution)/shard_map/kgts,skd->tkgd/dot_general | solution.py:92
  194.4 9.0 %fusion.46 = f32[256,8192]{1,0:T(8,128)} fusion(bf16[256,512]{0,1:T(8,128)(2,1)S(1)} %bitcast.46, bf16[512,8192]{0,1:T(8,128)(2,1)} %bitcast.44), kind=kOutput, calls=%fused_computation.64 | convolution fusion | flops 2147483648 | bytes 17039360 | tf_op jit(solution)/shard_map/dot_general | solution.py:128
  203.5 6.5 %convert_element_type.41 = f32[256,8192]{1,0:T(8,128)} convert(bf16[256,8192]{1,0:T(8,128)(2,1)} %param.9) | non-fusion elementwise | flops 2097152 | bytes 12582912 | tf_op jit(solution)/shard_map/convert_element_type | solution.py:112
  209.9 83.9 %reduce-scatter.2.cloned.1.call-done = f32[256,1024]{1,0:T(8,128)} async-done(((f32[256,8192]{1,0:T(8,128)}), f32[256,1024]{1,0:T(8,128)}) %reduce-scatter.2.cloned.1.call-update) | async-done | bytes 1048592 | tf_op jit(solution)/shard_map/reduce_scatter | solution.py:133
  293.8 2.5 fusion.19
  296.4 0.6 broadcast_in_dim.15
  297.0 3.3 %all-to-all-start = ((f32[8,1,512]{2,1,0:T(1,128)}), f32[8,1,512]{2,1,0:T(1,128)S(1)}, u32[]{:S(2)}, u32[]{:S(2)}) async-start(f32[8,1,512]{2,1,0:T(1,128)} %broadcast_in_dim.15), calls=%async_computation.1 | async-start | bytes 32768 | tf_op jit(solution)/shard_map/all_to_all | solution.py:24
  300.3 6.1 %all-to-all-done = f32[8,1,512]{2,1,0:T(1,128)S(1)} async-done(((f32[8,1,512]{2,1,0:T(1,128)}), f32[8,1,512]{2,1,0:T(1,128)S(1)}, u32[]{:S(2)}, u32[]{:S(2)}) %all-to-all-start) | async-done | bytes 16416 | tf_op jit(solution)/shard_map/all_to_all | solution.py:24
  306.5 0.6 rsqrt_multiply_fusion
  (25 shorter events, 1.1 us)
Async XLA Ops:
  7.2 78.6 %all-gather.6.cloned.1.call-start = ((), (), s32[]{:S(2)}) async-start(), calls=%async_computation.4 | async-start | bytes 8912896 | tf_op jit(solution)/shard_map/all_gather | solution.py:130
  7.9 168.6 %all-gather.4.cloned.1.call-start = ((), (), s32[]{:S(2)}) async-start(), calls=%async_computation.2 | async-start | bytes 13369344 | tf_op jit(solution)/shard_map/all_gather | solution.py:15
  10.1 283.7 %reduce-scatter.2.cloned.1.call-start = ((), (), s32[]{:S(2)}) async-start(), calls=%async_computation.3 | async-start | bytes 9437184 | tf_op jit(solution)/shard_map/reduce_scatter | solution.py:133
  85.8 90.8 %copy-start.2 = (f32[8192]{0:T(1024)S(1)}, f32[8192]{0:T(1024)}, u32[]{:S(2)}) copy-start(f32[8192]{0:T(1024)} %param.11) | copy-start | bytes 98308
  203.4 6.5 %copy-start = (f32[1024]{0:T(1024)S(1)}, f32[1024]{0:T(1024)}, u32[]{:S(2)}) copy-start(f32[1024]{0:T(1024)} %param.16) | copy-start | bytes 12292
  203.4 6.5 %copy-start.1 = (f32[1024]{0:T(1024)S(1)}, f32[1024]{0:T(1024)}, u32[]{:S(2)}) copy-start(f32[1024]{0:T(1024)} %param.17) | copy-start | bytes 12292
  297.0 9.5 %all-to-all-start = ((f32[8,1,512]{2,1,0:T(1,128)}), f32[8,1,512]{2,1,0:T(1,128)S(1)}, u32[]{:S(2)}, u32[]{:S(2)}) async-start(f32[8,1,512]{2,1,0:T(1,128)} %broadcast_in_dim.15), calls=%async_computation.1 | async-start | bytes 32768 | tf_op jit(solution)/shard_map/all_to_all | solution.py:24
Sparse Core Ops, SparseCore 0:
  10.4 75.3 all-gather.5
  88.3 88.2 all-gather.3
  203.6 90.2 reduce-scatter.1
